TPU v7x, 128 devices: a whole 4x4x4 slice. The times are simulated.
128 devices in a mesh: view: 4 (over z_hi, core), depth: 32 (over z_lo, y, x).
Axes of the slice: x: 4, y: 4, z: 4 (z_hi: 2, z_lo: 2; z = z_hi * 2 + z_lo), core: 2. Of those that a mesh axis runs over, the one named last changes fastest.
Arguments:
- volume: float32 [512, 128, 2048], P(('view', 'depth')), may hold values from -6 to 6
- step_weights: float32 [4, 8, 64], P('view'), may hold values from -0.75 to 0.75
- row_interp: float32 [4, 64, 64], P('view'), may hold values from -0.75 to 0.75
- col_interp: float32 [4, 64, 64], P('view'), may hold values from -0.75 to 0.75
- tf_table: float32 [8, 8], replicated, may hold values from -3 to 3
- materials: int32 [8, 2, 32], P(None, None, 'depth'), may hold values from 0 to 7
- entry: int32 [4, 512, 128], P('view'), may hold values from 0 to 15
Outputs:
- picture: float32 [4, 3, 512, 128], P('view', None, 'depth')
All inputs are finite; a program needn't handle non-finite values.
Results may differ from a plain program's by a relative error of at most 0.00018.
Values sent between devices are 32-bit elements; how exact they have to be, the bound alone decides.
A program may use at most 64 MiB of HBM per device.

v0:
```python
import jax
import jax.numpy as jnp
from jax import lax
from jax.sharding import Mesh
from jax.sharding import PartitionSpec as P

DEPTH = ("depth_0", "depth_1", "depth_2")
VIEW_DEPTH = ("view", "depth_0", "depth_1", "depth_2")


def nothing_yet(shard, identity):
    return jnp.broadcast_to(jnp.asarray(identity, shard.dtype), shard.shape)


def carried_in(shard, axes, combine, identity):
    before = start = nothing_yet(shard, identity)
    total = shard
    for axis in reversed(axes):
        peers, index = (lax.axis_size(axis), lax.axis_index(axis))
        pieces = lax.all_gather(total, axis)
        inside, total = (start, start)
        for k in range(peers):
            passed = k < index
            total = combine(total, pieces[k])
            inside = jnp.where(passed, total, inside)
        before = combine(inside, before)
    return before


def in_blocks(shard, dim, peers):
    dims = shard.shape
    blocks = shard.reshape(*dims[:dim], peers, dims[dim] // peers, *dims[dim + 1 :])
    return jnp.moveaxis(blocks, dim, 0)


def summed_on_arrival(shard, axis, dim):
    peers = lax.axis_size(axis)
    blocks = lax.all_to_all(in_blocks(shard, dim, peers), axis, 0, 0, tiled=True)
    return jnp.sum(blocks, axis=0)


def finish_brick(first, rows_map, cols_map):
    highest = lax.Precision.HIGHEST
    edge = rows_map.shape[0]
    count_steps, total_rows, total_cols = first.shape
    second = first.reshape(count_steps, total_rows // edge, edge, total_cols)
    second = jnp.einsum("stky,rk->stry", second, rows_map, precision=highest)
    third = second.reshape(count_steps, total_rows, total_cols // edge, edge)
    third = jnp.einsum("szuj,cj->szuc", third, cols_map, precision=highest)
    return third.reshape(count_steps, total_rows, total_cols)


def expand_classes(classes, tf_table, edge):
    choices_range = jnp.arange(tf_table.shape[0], dtype=jnp.int32)
    onehot = (classes[:, :, None] == choices_range).astype(jnp.float32)
    tiles = jnp.einsum("abm,mc->cab", onehot, tf_table, precision=lax.Precision.HIGHEST)
    count_coef, tiles_rows, tiles_cols = tiles.shape
    spread = jnp.broadcast_to(
        tiles[:, :, None, :, None], (count_coef, tiles_rows, edge, tiles_cols, edge)
    )
    return spread.reshape(count_coef, tiles_rows * edge, tiles_cols * edge)


def shade(samples, coefficients, live_mask, step_length):
    emission = jax.nn.softplus(coefficients[0:3, None] * samples[None] + coefficients[3:6, None])
    tau = (
        step_length
        * live_mask[None]
        * jax.nn.softplus(coefficients[6][None] * samples + coefficients[7][None])
    )
    earlier = jnp.cumsum(tau, axis=0) - tau
    weights = jnp.exp(-earlier) * (1.0 - jnp.exp(-tau))
    colours = jnp.sum(weights[None] * emission, axis=1)
    passed = jnp.exp(-jnp.sum(tau, axis=0))
    return (colours, passed)


def multiply(earlier, later):
    return earlier * later


def shards(volume, step_weights, row_interp, col_interp, tf_table, materials, entry):
    view_count = lax.axis_size("view")
    depth_count = lax.axis_size(DEPTH)
    depth_index = lax.axis_index(DEPTH)
    planes, lateral, span_cells = volume.shape
    brick_edge = span_cells // depth_count
    all_weights = lax.all_gather(step_weights, "view", axis=0, tiled=True)
    count_steps = all_weights.shape[1]
    cells = volume.reshape(planes, lateral, depth_count, brick_edge)
    contracted = jnp.einsum("zybi,gsi->gbszy", cells, all_weights, precision=lax.Precision.HIGHEST)
    contracted = contracted.reshape(view_count * depth_count, count_steps, planes, lateral)
    received = lax.all_to_all(contracted, VIEW_DEPTH, split_axis=0, concat_axis=2, tiled=True)
    samples = finish_brick(received[0], row_interp[0], col_interp[0])
    coefficients = expand_classes(materials[:, :, 0], tf_table, brick_edge)
    live_mask = (entry[0] <= depth_index).astype(jnp.float32)
    step_length = 2.0 / (samples.shape[0] * depth_count)
    colours, passed = shade(samples, coefficients, live_mask, step_length)
    before = carried_in(passed, DEPTH, multiply, jnp.ones_like(passed))
    terms = before[None] * colours
    rows_part = summed_on_arrival(terms, DEPTH, 1)
    return rows_part[None]


def solution(mesh):
    torus = Mesh(
        mesh.devices.reshape(mesh.shape["view"], 2, 4, 4), ("view", "depth_0", "depth_1", "depth_2")
    )
    return jax.shard_map(
        shards,
        mesh=torus,
        in_specs=(
            P(VIEW_DEPTH, None, None),
            P("view", None, None),
            P("view", None, None),
            P("view", None, None),
            P(),
            P(None, None, DEPTH),
            P("view", None, None),
        ),
        out_specs=P("view", None, DEPTH, None),
        check_vma=False,
    )
```

profile of v0, /device:TPU:0, one launch (start us, length us, event | category | flops | bytes accessed | tf_op | source)
XLA Modules:
  0.0 162.9 jit_solution(9018118237173368795)
XLA Ops:
  6.5 5.4 %copy.64 = f32[4,128,2048]{1,2,0:T(8,128)} copy(f32[4,128,2048]{2,1,0:T(8,128)} %param.7) | data formatting | bytes 8388608 | tf_op args[0]
  11.9 7.2 %all_gather.15 = f32[4,8,64]{2,1,0:T(8,128)S(1)} all-gather(f32[1,8,64]{2,1,0:T(8,128)S(1)} %copy-done.6), channel_id=1, replica_groups=mesh['view'=4,'depth_0'=2,'depth_1'=4,'depth_2'=4] {'view'}, dimensions={0}, use_global_device_ids=true | all-gather | bytes 10240 | tf_op jit(solution)/shard_map/all_gather | solution.py:88
  19.1 3.9 %convolution_bitcast_fusion.1 = f32[4,32,8,4,128]{4,2,1,3,0:T(8,128)S(1)} fusion(f32[4,128,32,64,1]{1,3,2,0,4:T(8,128)} %bitcast.69, f32[4,8,64]{2,1,0:T(8,128)S(1)} %all_gather.15), kind=kOutput, calls=%fused_computation.13 | convolution fusion | flops 402653184 | bytes 6299648 | tf_op jit(solution)/shard_map/zybi,gsi->gbszy/dot_general | solution.py:91
  23.0 1.6 %copy.65 = f32[4,32,8,4,128]{4,2,3,1,0:T(8,128)} copy(f32[4,32,8,4,128]{4,2,1,3,0:T(8,128)S(1)} %convolution_bitcast_fusion.1) | data formatting | bytes 4194304 | tf_op jit(solution)/shard_map/zybi,gsi->gbszy/transpose | solution.py:91
  24.6 10.6 %all-to-all-start = ((f32[128,8,4,128]{3,1,2,0:T(8,128)}), f32[128,8,4,128]{3,1,2,0:T(8,128)S(1)}, u32[]{:S(2)}, u32[]{:S(2)}) async-start(f32[128,8,4,128]{3,1,2,0:T(8,128)} %bitcast.71), calls=%async_computation | async-start | bytes 4194304 | tf_op jit(solution)/shard_map/all_to_all | solution.py:93
  36.3 28.8 %all-to-all-done = f32[128,8,4,128]{3,1,2,0:T(8,128)S(1)} async-done(((f32[128,8,4,128]{3,1,2,0:T(8,128)}), f32[128,8,4,128]{3,1,2,0:T(8,128)S(1)}, u32[]{:S(2)}, u32[]{:S(2)}) %all-to-all-start) | async-done | bytes 2097184 | tf_op jit(solution)/shard_map/all_to_all | solution.py:93
  65.8 2.0 %convolution_bitcast_fusion = f32[8,8,64,128]{3,2,1,0:T(8,128)S(1)} fusion(f32[8,8,64,128]{3,2,1,0:T(8,128)S(1)} %bitcast.72, f32[1,64,64]{2,1,0:T(8,128)S(1)} %copy-done.5), kind=kOutput, calls=%fused_computation.12 | convolution fusion | flops 402653184 | bytes 4210688 | tf_op jit(solution)/shard_map/stky,rk->stry/dot_general | solution.py:47
  67.8 3.7 %reshape.111 = f32[8,512,2,64]{3,2,1,0:T(2,128)} reshape(f32[8,8,64,128]{3,2,1,0:T(8,128)S(1)} %convolution_bitcast_fusion) | data formatting | bytes 4194304 | tf_op jit(solution)/shard_map/reshape | solution.py:48
  71.5 7.0 %fusion.10 = (u8[512,2,64]{0,2,1:T(8,128)(4,1)S(1)}, f32[8,512,2,64]{1,3,2,0:T(8,128)S(1)}) fusion(f32[512,2]{0,1:T(2,128)S(1)} %broadcast_in_dim.39, f32[512,2]{0,1:T(2,128)S(1)} %broadcast_in_dim.37, f32[1,64,64]{2,1,0:T(8,128)S(1)} %copy-done, f32[8,512,2,64]{3,2,1,0:T(2,128)} %reshape.111), kind=kOutput, calls=%fused_computation.20 | convolution fusion | flops 406257664 | bytes 4284416 | tf_op jit(solution)/shard_map/szuj,cj->szuc/dot_general | solution.py:49
  78.5 1.4 multiply_reduce_fusion
  80.0 0.8 copy.68
  81.2 20.0 %all-gather.3.cloned.1.call-done = f32[4,512,128]{2,1,0:T(8,128)} async-done(((f32[1,512,128]{2,1,0:T(8,128)}), f32[4,512,128]{2,1,0:T(8,128)}) %all-gather.3.cloned.1.call-update) | async-done | bytes 1048592 | tf_op jit(solution)/shard_map/all_gather | solution.py:20
  101.1 1.9 %slice_multiply_fusion.4 = f32[1,512,128]{2,1,0:T(8,128)} fusion(f32[4,512,128]{2,1,0:T(8,128)} %all-gather.3.cloned.1.call-done), kind=kLoop, calls=%fused_computation.27 | loop fusion | flops 196608 | bytes 1310720 | tf_op jit(solution)/shard_map/mul | solution.py:79
  103.7 1.6 %broadcast_in_dim.46 = f32[3,8,64,2,64]{4,3,2,1,0:T(2,128)} broadcast(f32[3,8,2]{2,1,0:T(8,128)S(1)} %copy.72), dimensions={0,1,3} | broadcast | bytes 786624 | tf_op jit(solution)/shard_map/broadcast_in_dim | solution.py:58
  105.4 3.1 %add.64 = f32[3,512,128]{2,1,0:T(8,128)} reshape(f32[3,8,64,2,64]{4,3,2,1,0:T(2,128)} %broadcast_in_dim.46) | data formatting | bytes 1572864 | tf_op jit(solution)/shard_map/add | solution.py:65
  108.5 1.6 %broadcast_in_dim.45 = f32[3,8,64,2,64]{4,3,2,1,0:T(2,128)} broadcast(f32[3,8,2]{2,1,0:T(8,128)S(1)} %copy.70), dimensions={0,1,3} | broadcast | bytes 786624 | tf_op jit(solution)/shard_map/broadcast_in_dim | solution.py:58
  110.2 3.0 %mul.170 = f32[3,512,128]{2,1,0:T(8,128)} reshape(f32[3,8,64,2,64]{4,3,2,1,0:T(2,128)} %broadcast_in_dim.45) | data formatting | bytes 1572864 | tf_op jit(solution)/shard_map/mul | solution.py:65
  113.2 1.8 %copy.71 = f32[8,512,128]{2,1,0:T(8,128)} copy(f32[8,512,128]{1,2,0:T(8,128)S(1)} %bitcast.67) | data formatting | bytes 4194304 | tf_op jit(solution)/shard_map/reshape | solution.py:50
  115.0 4.2 %subtract_multiply_fusion = f32[8,512,128]{1,2,0:T(8,128)} fusion(f32[8,512,128]{1,2,0:T(8,128)S(1)} %bitcast.68, f32[512,128]{0,1:T(8,128)S(1)} %broadcast_in_dim.44, f32[512,128]{0,1:T(8,128)S(1)} %broadcast_in_dim.42, f32[512,128]{0,1:T(8,128)S(1)} %fusion.23), kind=kOutput, calls=%fused_computation.9 | output fusion | flops 15728640 | bytes 4980736 | tf_op jit(solution)/shard_map/jit(cumsum)/reduce_window_sum | solution.py:71
  119.2 3.1 %copy.69 = f32[8,512,128]{2,1,0:T(8,128)} copy(f32[8,512,128]{1,2,0:T(8,128)} %subtract_multiply_fusion) | data formatting | bytes 4194304 | tf_op jit(solution)/shard_map/mul | solution.py:72
  122.3 5.7 %fusion.1 = f32[3,512,128]{2,1,0:T(8,128)S(1)} fusion(f32[3,512,128]{2,1,0:T(8,128)} %add.64, f32[8,512,128]{2,1,0:T(8,128)S(1)} %copy-done.1, f32[3,512,128]{2,1,0:T(8,128)} %mul.170, f32[8,512,128]{2,1,0:T(8,128)} %copy.69), kind=kLoop, calls=%fused_computation.2 | loop fusion | flops 15532032 | bytes 6553600 | tf_op jit(solution)/shard_map/reduce_sum | solution.py:73
  128.0 1.4 slice_multiply_fusion.1
  129.4 7.0 %all_gather.18 = f32[2,512,128]{2,1,0:T(8,128)S(1)} all-gather(f32[1,512,128]{2,1,0:T(8,128)S(1)} %slice_multiply_fusion.1), channel_id=1, replica_groups=mesh['view'=4,'depth_0'=2,'depth_1'=4,'depth_2'=4] {'depth_0'}, dimensions={0}, use_global_device_ids=true | all-gather | bytes 786432 | tf_op jit(solution)/shard_map/all_gather | solution.py:20
  136.8 18.6 %all_to_all.20 = f32[32,3,16,128]{3,2,1,0:T(8,128)S(1)} all-to-all(f32[32,3,16,128]{3,2,1,0:T(8,128)S(1)} %copy.73), channel_id=1, replica_groups=mesh['view'=4,'depth_0'=2,'depth_1'=4,'depth_2'=4] {'depth_0','depth_1',..., dimensions={0} | all-to-all | bytes 1572864 | tf_op jit(solution)/shard_map/all_to_all | solution.py:38
  (45 shorter events, 3.7 us)
Async XLA Ops:
  6.5 65.0 %copy-start = (f32[1,64,64]{2,1,0:T(8,128)S(1)}, f32[1,64,64]{2,1,0:T(8,128)}, u32[]{:S(2)}) copy-start(f32[1,64,64]{2,1,0:T(8,128)} %param.10) | copy-start | bytes 49156
  6.5 5.4 %copy-start.6 = (f32[1,8,64]{2,1,0:T(8,128)S(1)}, f32[1,8,64]{2,1,0:T(8,128)}, u32[]{:S(2)}) copy-start(f32[1,8,64]{2,1,0:T(8,128)} %param.8) | copy-start | bytes 6148
  24.6 10.9 %copy-start.4 = (s32[1,512,128]{2,1,0:T(8,128)S(1)}, s32[1,512,128]{2,1,0:T(8,128)}, u32[]{:S(2)}) copy-start(s32[1,512,128]{2,1,0:T(8,128)} %param.13) | copy-start | bytes 786436
  24.6 11.0 %copy-start.7 = (f32[8,8]{1,0:T(8,128)S(1)}, f32[8,8]{1,0:T(8,128)}, u32[]{:S(2)}) copy-start(f32[8,8]{1,0:T(8,128)} %param.11) | copy-start | bytes 772
  24.6 11.0 %copy-start.8 = (s32[8,2,1]{0,2,1:T(1,128)S(1)}, s32[8,2,1]{0,2,1:T(1,128)}, u32[]{:S(2)}) copy-start(s32[8,2,1]{0,2,1:T(1,128)} %param.12) | copy-start | bytes 196
  24.6 40.4 %all-to-all-start = ((f32[128,8,4,128]{3,1,2,0:T(8,128)}), f32[128,8,4,128]{3,1,2,0:T(8,128)S(1)}, u32[]{:S(2)}, u32[]{:S(2)}) async-start(f32[128,8,4,128]{3,1,2,0:T(8,128)} %bitcast.71), calls=%async_computation | async-start | bytes 4194304 | tf_op jit(solution)/shard_map/all_to_all | solution.py:93
  35.3 65.9 %all-gather.3.cloned.1.call-start = ((), (), s32[]{:S(2)}) async-start(), calls=%async_computation.2 | async-start | bytes 1310720 | tf_op jit(solution)/shard_map/all_gather | solution.py:20
  65.0 0.8 copy-start.5
  80.9 47.1 %all-gather.5.cloned.1.call-start = ((), (), s32[]{:S(2)}) async-start(), calls=%async_computation.3 | async-start | bytes 1310720 | tf_op jit(solution)/shard_map/all_gather | solution.py:20
  119.2 3.1 %copy-start.1 = (f32[8,512,128]{2,1,0:T(8,128)S(1)}, f32[8,512,128]{2,1,0:T(8,128)}, u32[]{:S(2)}) copy-start(f32[8,512,128]{2,1,0:T(8,128)} %copy.71) | copy-start | bytes 6291460
  128.0 8.5 %copy-start.2 = (f32[4,512,128]{2,1,0:T(8,128)S(1)}, f32[4,512,128]{2,1,0:T(8,128)}, u32[]{:S(2)}) copy-start(f32[4,512,128]{2,1,0:T(8,128)} %all-gather.3.cloned.1.call-done) | copy-start | bytes 3145732
  128.0 8.4 %copy-start.3 = (f32[4,512,128]{2,1,0:T(8,128)S(1)}, f32[4,512,128]{2,1,0:T(8,128)}, u32[]{:S(2)}) copy-start(f32[4,512,128]{2,1,0:T(8,128)} %all-gather.5.cloned.1.call-done) | copy-start | bytes 3145732
Sparse Core Ops, SparseCore 0:
  81.0 20.0 all-gather.2
  103.2 24.4 all-gather.4
where the time goes:
time: 163 us
  waiting for transfers between devices  48.8 us (30%)
  blocking collectives  32.9 us (20%)
  local copies, waits for them, and re-layouts  27.7 us (17%)
  other arithmetic  15.6 us (10%)
  between operations  13.6 us (8%)
  matrix products  13.1 us (8%)
  starting transfers between devices  11.1 us (7%)
    all_to_all x1, waiting for transfers between devices, shards(): lax.all_to_all(contracted, VIEW_DEPTH, split_axis=0, concat_axis=2, tiled...  28.8 us
    all_gather x2, waiting for transfers between devices, carried_in(): pieces = lax.all_gather(total, axis)  20 us
    all_to_all x1, blocking collectives, summed_on_arrival(): lax.all_to_all(in_blocks(shard, dim, peers), axis, 0, 0, tiled=True)  18.6 us
    all_to_all x1, starting transfers between devices, shards(): lax.all_to_all(contracted, VIEW_DEPTH, split_axis=0, concat_axis=2, tiled...  10.6 us
    all_gather x1, blocking collectives, shards(): all_weights = lax.all_gather(step_weights, 'view', axis=0, tiled=True)  7.25 us
    dot_general x1, matrix products, finish_brick(): third = jnp.einsum('szuj,cj->szuc', third, cols_map, precision=highest)  7.04 us
    all_gather x1, blocking collectives, carried_in(): pieces = lax.all_gather(total, axis)  7.04 us
    unnamed x20, local copies, waits for them, and re-layouts  5.73 us
  transfers between devices with their start and end apart: 3, of which 2 were waited for; matrix products, arithmetic and copies ran while one was open for 16% of the time, Pallas kernels for 0%

commit v1 on v0

--- a/solution.py
+++ b/solution.py
@@ -85,7 +85,9 @@
     depth_index = lax.axis_index(DEPTH)
     planes, lateral, span_cells = volume.shape
     brick_edge = span_cells // depth_count
-    all_weights = lax.all_gather(step_weights, "view", axis=0, tiled=True)
+    all_weights = jnp.concatenate(
+        lax.all_to_all(jnp.stack([step_weights] * lax.axis_size("view")), "view", 0, 0), axis=0
+    )
     count_steps = all_weights.shape[1]
     cells = volume.reshape(planes, lateral, depth_count, brick_edge)
     contracted = jnp.einsum("zybi,gsi->gbszy", cells, all_weights, precision=lax.Precision.HIGHEST)

time: 163 us -> 164 us (level)
  blocking collectives: 32.9 us -> 25.7 us
  starting transfers between devices: 11.1 us -> 16.5 us
  local copies, waits for them, and re-layouts: 27.7 us -> 29.7 us
    all_gather x1 -> x0, blocking collectives: 7.25 us -> none  [shards(): all_weights = lax.all_gather(step_weights, 'view', axis=0, tiled=True)]
    all_to_all x0 -> x1, starting transfers between devices: none -> 5.26 us  [shards(): lax.all_to_all(jnp.stack([step_weights] * lax.axis_size('view')), 'view',...]
  transfers between devices with their start and end apart: 3 -> 4, of which waited for: 2 -> 2; matrix products, arithmetic and copies ran while one was open for 16% -> 19% of each run, Pallas kernels for 0% -> 0%
where the time goes in v1:
time: 164 us
  waiting for transfers between devices  48.8 us (30%)
  local copies, waits for them, and re-layouts  29.7 us (18%)
  blocking collectives  25.7 us (16%)
  starting transfers between devices  16.5 us (10%)
  other arithmetic  16.3 us (10%)
  between operations  13.6 us (8%)
  matrix products  13.1 us (8%)
    all_to_all x1, waiting for transfers between devices, shards(): lax.all_to_all(contracted, VIEW_DEPTH, split_axis=0, concat_axis=2, tiled...  28.8 us
    all_gather x2, waiting for transfers between devices, carried_in(): pieces = lax.all_gather(total, axis)  20 us
    all_to_all x1, blocking collectives, summed_on_arrival(): lax.all_to_all(in_blocks(shard, dim, peers), axis, 0, 0, tiled=True)  18.6 us
    all_to_all x1, starting transfers between devices, shards(): lax.all_to_all(contracted, VIEW_DEPTH, split_axis=0, concat_axis=2, tiled...  10.7 us
    all_gather x1, blocking collectives, carried_in(): pieces = lax.all_gather(total, axis)  7.04 us
    dot_general x1, matrix products, finish_brick(): third = jnp.einsum('szuj,cj->szuc', third, cols_map, precision=highest)  7.04 us
    unnamed x20, local copies, waits for them, and re-layouts  6.51 us
    reduce_sum x1, other arithmetic, shade(): colours = jnp.sum(weights[None] * emission, axis=1)  5.66 us
  transfers between devices with their start and end apart: 4, of which 2 were waited for; matrix products, arithmetic and copies ran while one was open for 19% of the time, Pallas kernels for 0%

profile of v1, /device:TPU:0, one launch (start us, length us, event | category | flops | bytes accessed | tf_op | source)
XLA Modules:
  0.0 163.7 jit_solution(14250828601573525158)
XLA Ops:
  7.9 5.3 %all-to-all-start = ((f32[4,1,512]{2,1,0:T(1,128)}), f32[4,1,512]{2,1,0:T(1,128)S(1)}, u32[]{:S(2)}, u32[]{:S(2)}) async-start(f32[4,1,512]{2,1,0:T(1,128)} %reshape.119), calls=%async_computation | async-start | bytes 16384 | tf_op jit(solution)/shard_map/all_to_all | solution.py:89
  13.2 5.4 %copy.64 = f32[4,128,2048]{1,2,0:T(8,128)} copy(f32[4,128,2048]{2,1,0:T(8,128)} %param.7) | data formatting | bytes 8388608 | tf_op args[0]
  19.8 3.9 %convolution_bitcast_fusion.1 = f32[4,32,8,4,128]{4,2,1,3,0:T(8,128)S(1)} fusion(f32[4,128,32,64,1]{1,3,2,0,4:T(8,128)} %bitcast.72, f32[4,1,8,64]{3,2,1,0:T(8,128)S(1)} %reshape.120), kind=kOutput, calls=%fused_computation.13 | convolution fusion | flops 402653184 | bytes 6299648 | tf_op jit(solution)/shard_map/zybi,gsi->gbszy/dot_general | solution.py:93
  23.7 1.6 copy.65
  25.3 10.7 %all-to-all-start.1 = ((f32[128,8,4,128]{3,1,2,0:T(8,128)}), f32[128,8,4,128]{3,1,2,0:T(8,128)S(1)}, u32[]{:S(2)}, u32[]{:S(2)}) async-start(f32[128,8,4,128]{3,1,2,0:T(8,128)} %bitcast.74), calls=%async_computation.1 | async-start | bytes 4194304 | tf_op jit(solution)/shard_map/all_to_all | solution.py:95
  37.0 28.8 %all-to-all-done.1 = f32[128,8,4,128]{3,1,2,0:T(8,128)S(1)} async-done(((f32[128,8,4,128]{3,1,2,0:T(8,128)}), f32[128,8,4,128]{3,1,2,0:T(8,128)S(1)}, u32[]{:S(2)}, u32[]{:S(2)}) %all-to-all-start.1) | async-done | bytes 2097184 | tf_op jit(solution)/shard_map/all_to_all | solution.py:95
  66.6 2.0 %convolution_bitcast_fusion = f32[8,8,64,128]{3,2,1,0:T(8,128)S(1)} fusion(f32[8,8,64,128]{3,2,1,0:T(8,128)S(1)} %bitcast.75, f32[1,64,64]{2,1,0:T(8,128)S(1)} %copy-done.5), kind=kOutput, calls=%fused_computation.12 | convolution fusion | flops 402653184 | bytes 4210688 | tf_op jit(solution)/shard_map/stky,rk->stry/dot_general | solution.py:47
  68.6 3.7 %reshape.118 = f32[8,512,2,64]{3,2,1,0:T(2,128)} reshape(f32[8,8,64,128]{3,2,1,0:T(8,128)S(1)} %convolution_bitcast_fusion) | data formatting | bytes 4194304 | tf_op jit(solution)/shard_map/reshape | solution.py:48
  72.3 7.0 %fusion.10 = (u8[512,2,64]{0,2,1:T(8,128)(4,1)S(1)}, f32[8,512,2,64]{1,3,2,0:T(8,128)S(1)}) fusion(f32[512,2]{0,1:T(2,128)S(1)} %broadcast_in_dim.39, f32[512,2]{0,1:T(2,128)S(1)} %broadcast_in_dim.37, f32[1,64,64]{2,1,0:T(8,128)S(1)} %copy-done, f32[8,512,2,64]{3,2,1,0:T(2,128)} %reshape.118), kind=kOutput, calls=%fused_computation.20 | convolution fusion | flops 406257664 | bytes 4284416 | tf_op jit(solution)/shard_map/szuj,cj->szuc/dot_general | solution.py:49
  79.3 1.4 multiply_reduce_fusion
  80.8 0.8 copy.68
  81.9 20.0 %all-gather.3.cloned.1.call-done = f32[4,512,128]{2,1,0:T(8,128)} async-done(((f32[1,512,128]{2,1,0:T(8,128)}), f32[4,512,128]{2,1,0:T(8,128)}) %all-gather.3.cloned.1.call-update) | async-done | bytes 1048592 | tf_op jit(solution)/shard_map/all_gather | solution.py:20
  101.9 1.9 %slice_multiply_fusion.4 = f32[1,512,128]{2,1,0:T(8,128)} fusion(f32[4,512,128]{2,1,0:T(8,128)} %all-gather.3.cloned.1.call-done), kind=kLoop, calls=%fused_computation.27 | loop fusion | flops 196608 | bytes 1310720 | tf_op jit(solution)/shard_map/mul | solution.py:79
  104.5 1.6 %broadcast_in_dim.46 = f32[3,8,64,2,64]{4,3,2,1,0:T(2,128)} broadcast(f32[3,8,2]{2,1,0:T(8,128)S(1)} %copy.72), dimensions={0,1,3} | broadcast | bytes 786624 | tf_op jit(solution)/shard_map/broadcast_in_dim | solution.py:58
  106.1 3.1 %add.64 = f32[3,512,128]{2,1,0:T(8,128)} reshape(f32[3,8,64,2,64]{4,3,2,1,0:T(2,128)} %broadcast_in_dim.46) | data formatting | bytes 1572864 | tf_op jit(solution)/shard_map/add | solution.py:65
  109.3 1.6 %broadcast_in_dim.45 = f32[3,8,64,2,64]{4,3,2,1,0:T(2,128)} broadcast(f32[3,8,2]{2,1,0:T(8,128)S(1)} %copy.70), dimensions={0,1,3} | broadcast | bytes 786624 | tf_op jit(solution)/shard_map/broadcast_in_dim | solution.py:58
  111.0 3.0 %mul.170 = f32[3,512,128]{2,1,0:T(8,128)} reshape(f32[3,8,64,2,64]{4,3,2,1,0:T(2,128)} %broadcast_in_dim.45) | data formatting | bytes 1572864 | tf_op jit(solution)/shard_map/mul | solution.py:65
  114.0 1.8 %copy.71 = f32[8,512,128]{2,1,0:T(8,128)} copy(f32[8,512,128]{1,2,0:T(8,128)S(1)} %bitcast.70) | data formatting | bytes 4194304 | tf_op jit(solution)/shard_map/reshape | solution.py:50
  115.8 4.2 %subtract_multiply_fusion = f32[8,512,128]{1,2,0:T(8,128)} fusion(f32[8,512,128]{1,2,0:T(8,128)S(1)} %bitcast.71, f32[512,128]{0,1:T(8,128)S(1)} %broadcast_in_dim.44, f32[512,128]{0,1:T(8,128)S(1)} %broadcast_in_dim.42, f32[512,128]{0,1:T(8,128)S(1)} %fusion.23), kind=kOutput, calls=%fused_computation.9 | output fusion | flops 15728640 | bytes 4980736 | tf_op jit(solution)/shard_map/jit(cumsum)/reduce_window_sum | solution.py:71
  120.0 3.1 %copy.69 = f32[8,512,128]{2,1,0:T(8,128)} copy(f32[8,512,128]{1,2,0:T(8,128)} %subtract_multiply_fusion) | data formatting | bytes 4194304 | tf_op jit(solution)/shard_map/mul | solution.py:72
  123.1 5.7 %fusion.1 = f32[3,512,128]{2,1,0:T(8,128)S(1)} fusion(f32[3,512,128]{2,1,0:T(8,128)} %add.64, f32[8,512,128]{2,1,0:T(8,128)S(1)} %copy-done.1, f32[3,512,128]{2,1,0:T(8,128)} %mul.170, f32[8,512,128]{2,1,0:T(8,128)} %copy.69), kind=kLoop, calls=%fused_computation.2 | loop fusion | flops 15532032 | bytes 6553600 | tf_op jit(solution)/shard_map/reduce_sum | solution.py:73
  128.8 1.4 slice_multiply_fusion.1
  130.2 7.0 %all_gather.14 = f32[2,512,128]{2,1,0:T(8,128)S(1)} all-gather(f32[1,512,128]{2,1,0:T(8,128)S(1)} %slice_multiply_fusion.1), channel_id=1, replica_groups=mesh['view'=4,'depth_0'=2,'depth_1'=4,'depth_2'=4] {'depth_0'}, dimensions={0}, use_global_device_ids=true | all-gather | bytes 786432 | tf_op jit(solution)/shard_map/all_gather | solution.py:20
  137.6 18.6 %all_to_all.25 = f32[32,3,16,128]{3,2,1,0:T(8,128)S(1)} all-to-all(f32[32,3,16,128]{3,2,1,0:T(8,128)S(1)} %copy.73), channel_id=1, replica_groups=mesh['view'=4,'depth_0'=2,'depth_1'=4,'depth_2'=4] {'depth_0','depth_1',..., dimensions={0} | all-to-all | bytes 1572864 | tf_op jit(solution)/shard_map/all_to_all | solution.py:38
  (49 shorter events, 6.4 us)
Async XLA Ops:
  6.5 65.7 %copy-start = (f32[1,64,64]{2,1,0:T(8,128)S(1)}, f32[1,64,64]{2,1,0:T(8,128)}, u32[]{:S(2)}) copy-start(f32[1,64,64]{2,1,0:T(8,128)} %param.10) | copy-start | bytes 49156
  7.9 10.6 %all-to-all-start = ((f32[4,1,512]{2,1,0:T(1,128)}), f32[4,1,512]{2,1,0:T(1,128)S(1)}, u32[]{:S(2)}, u32[]{:S(2)}) async-start(f32[4,1,512]{2,1,0:T(1,128)} %reshape.119), calls=%async_computation | async-start | bytes 16384 | tf_op jit(solution)/shard_map/all_to_all | solution.py:89
  25.3 11.0 %copy-start.4 = (s32[1,512,128]{2,1,0:T(8,128)S(1)}, s32[1,512,128]{2,1,0:T(8,128)}, u32[]{:S(2)}) copy-start(s32[1,512,128]{2,1,0:T(8,128)} %param.13) | copy-start | bytes 786436
  25.3 11.1 %copy-start.6 = (f32[8,8]{1,0:T(8,128)S(1)}, f32[8,8]{1,0:T(8,128)}, u32[]{:S(2)}) copy-start(f32[8,8]{1,0:T(8,128)} %param.11) | copy-start | bytes 772
  25.3 11.1 %copy-start.7 = (s32[8,2,1]{0,2,1:T(1,128)S(1)}, s32[8,2,1]{0,2,1:T(1,128)}, u32[]{:S(2)}) copy-start(s32[8,2,1]{0,2,1:T(1,128)} %param.12) | copy-start | bytes 196
  25.3 40.5 %all-to-all-start.1 = ((f32[128,8,4,128]{3,1,2,0:T(8,128)}), f32[128,8,4,128]{3,1,2,0:T(8,128)S(1)}, u32[]{:S(2)}, u32[]{:S(2)}) async-start(f32[128,8,4,128]{3,1,2,0:T(8,128)} %bitcast.74), calls=%async_computation.1 | async-start | bytes 4194304 | tf_op jit(solution)/shard_map/all_to_all | solution.py:95
  36.0 65.9 %all-gather.3.cloned.1.call-start = ((), (), s32[]{:S(2)}) async-start(), calls=%async_computation.3 | async-start | bytes 1310720 | tf_op jit(solution)/shard_map/all_gather | solution.py:20
  65.8 0.8 copy-start.5
  81.7 47.2 %all-gather.5.cloned.1.call-start = ((), (), s32[]{:S(2)}) async-start(), calls=%async_computation.4 | async-start | bytes 1310720 | tf_op jit(solution)/shard_map/all_gather | solution.py:20
  120.0 3.1 %copy-start.1 = (f32[8,512,128]{2,1,0:T(8,128)S(1)}, f32[8,512,128]{2,1,0:T(8,128)}, u32[]{:S(2)}) copy-start(f32[8,512,128]{2,1,0:T(8,128)} %copy.71) | copy-start | bytes 6291460
  128.8 8.5 %copy-start.2 = (f32[4,512,128]{2,1,0:T(8,128)S(1)}, f32[4,512,128]{2,1,0:T(8,128)}, u32[]{:S(2)}) copy-start(f32[4,512,128]{2,1,0:T(8,128)} %all-gather.3.cloned.1.call-done) | copy-start | bytes 3145732
  128.8 8.4 %copy-start.3 = (f32[4,512,128]{2,1,0:T(8,128)S(1)}, f32[4,512,128]{2,1,0:T(8,128)}, u32[]{:S(2)}) copy-start(f32[4,512,128]{2,1,0:T(8,128)} %all-gather.5.cloned.1.call-done) | copy-start | bytes 3145732
Sparse Core Ops, SparseCore 0:
  81.8 20.0 all-gather.2
  104.0 24.4 all-gather.4
